TPU v7x, 128 devices: a whole 4x4x4 slice. The times are simulated.
128 devices in a mesh: section: 4 (over y), mp: 32 (over x, z, core).
Axes of the slice: x: 4, y: 4, z: 4, core: 2. Of those that a mesh axis runs over, the one named last changes fastest.
Arguments:
- hidden_in: bfloat16 [1, 4, 64, 4096], P(None, 'section'), may hold values from -36 to 36
- attn_gain: bfloat16 [4, 4096], P('section'), may hold values from 0.5 to 2
- w_query: bfloat16 [4, 4096, 4096], P('section', None, 'mp'), may hold values from -0.75 to 0.75
- w_key: bfloat16 [4, 4096, 1024], P('section', None, 'mp'), may hold values from -0.0625 to 0.0625
- w_value: bfloat16 [4, 4096, 1024], P('section', None, 'mp'), may hold values from -0.09375 to 0.09375
- w_out: bfloat16 [4, 4096, 4096], P('section', 'mp'), may hold values from -0.09375 to 0.09375
- ffn_gain: bfloat16 [4, 4096], P('section'), may hold values from 0.5 to 2
- w_gate: bfloat16 [4, 4096, 16384], P('section', None, 'mp'), may hold values from -0.09375 to 0.09375
- w_up: bfloat16 [4, 4096, 16384], P('section', None, 'mp'), may hold values from -0.09375 to 0.09375
- w_down: bfloat16 [4, 16384, 4096], P('section', 'mp'), may hold values from -0.046875 to 0.046875
- ffn_blocks: int32 [4, 4], P(None, 'section'), may hold values from 1 to 112
- heads_on: int32 [4, 4], P(None, 'section'), may hold values from 1 to 32
Outputs:
- hidden_out: bfloat16 [1, 4, 64, 4096], P(None, 'section')
Inputs may be any that keep to these rules, and one draw needn't show every extreme that they name: `ffn_blocks`: hidden units below 128 times the entry are active. `heads_on`: query heads below the entry are active.
All inputs are finite; a program needn't handle non-finite values.
Results may differ from a plain program's by a relative error of at most 0.025.
Values may be sent and summed in bfloat16 or wider, within the bound.
A program may use at most 128 MiB of HBM per device.

v0:
```python
import jax
import jax.numpy as jnp
from jax import lax
from jax.sharding import PartitionSpec as P

HEADS = 32
KV_HEADS = 8
HD = 128
BLOCK = 128
ROPE_BASE = 500000.0
EPSILON = 1e-05


def rows_first(arrays, axis, dims):
    turned = [jnp.moveaxis(a, dim, 0) for a, dim in zip(arrays, dims)]
    widths = [t[0].size for t in turned]
    both = jnp.concatenate([t.reshape(-1, w) for t, w in zip(turned, widths)], axis=1)
    out = lax.all_gather(both, axis, axis=0, tiled=True)
    pieces = jnp.split(out, [sum(widths[:k]) for k in range(1, len(widths))], axis=1)
    return tuple(
        (
            jnp.moveaxis(b.reshape(-1, *t.shape[1:]), 0, dim)
            for b, t, dim in zip(pieces, turned, dims)
        )
    )


def laid_out(pieces, dim):
    pieces = jnp.moveaxis(pieces, 0, dim)
    dims = pieces.shape
    return pieces.reshape(*dims[:dim], dims[dim] * dims[dim + 1], *dims[dim + 2 :])


def sent_to_all(array, axis):
    copies = jnp.broadcast_to(array, (lax.axis_size(axis), *array.shape))
    return lax.all_to_all(copies, axis, split_axis=0, concat_axis=0, tiled=True)


def collect(array, axis, dim):
    return laid_out(sent_to_all(array, axis), dim)


def in_blocks(array, dim, peers):
    dims = array.shape
    pieces = array.reshape(*dims[:dim], peers, dims[dim] // peers, *dims[dim + 1 :])
    return jnp.moveaxis(pieces, dim, 0)


def summed_on_arrival(array, axis, dim):
    peers = lax.axis_size(axis)
    pieces = lax.all_to_all(in_blocks(array, dim, peers), axis, 0, 0, tiled=True)
    return jnp.sum(pieces.astype(jnp.float32), axis=0)


def passed_along(array, axis, by):
    peers = lax.axis_size(axis)
    return lax.ppermute(array, axis, [(i, (i + by) % peers) for i in range(peers)])


def rms_scale(values, gain_row):
    mean_sq = jnp.mean(values * values, axis=-1, keepdims=True)
    return values * lax.rsqrt(mean_sq + EPSILON) * gain_row.astype(jnp.float32)


def rotate(values):
    length = values.shape[0]
    half_dim = values.shape[-1] // 2
    frequency = ROPE_BASE ** (-(jnp.arange(half_dim, dtype=jnp.float32) / half_dim))
    angles = jnp.arange(length, dtype=jnp.float32)[:, None] * frequency[None, :]
    cosine_table = jnp.cos(angles)[:, None, :]
    sine_table = jnp.sin(angles)[:, None, :]
    front_half = values[..., :half_dim].astype(jnp.float32)
    back_half = values[..., half_dim:].astype(jnp.float32)
    return jnp.concatenate(
        [
            front_half * cosine_table - back_half * sine_table,
            front_half * sine_table + back_half * cosine_table,
        ],
        axis=-1,
    )


def attend_local(projected, query_width, key_width, active, first_head):
    length = projected.shape[0]
    heads_here = query_width // HD
    group_size = HEADS // KV_HEADS
    queries = rotate(projected[:, :query_width].reshape(length, heads_here, HD)).astype(
        jnp.bfloat16
    )
    key_local = projected[:, query_width : query_width + key_width].astype(jnp.bfloat16)
    value_local = projected[:, query_width + key_width :].astype(jnp.bfloat16)
    key_whole, value_whole = rows_first((key_local, value_local), "mp", (1, 1))
    key_heads = key_whole.reshape(length, HD, KV_HEADS).transpose(0, 2, 1)
    value_heads = value_whole.reshape(length, HD, KV_HEADS).transpose(0, 2, 1)
    kv_here = max(1, heads_here // group_size)
    repeat_count = heads_here // kv_here
    first_kv = first_head // group_size
    key_pick = lax.dynamic_slice_in_dim(key_heads, first_kv, kv_here, 1)
    value_pick = lax.dynamic_slice_in_dim(value_heads, first_kv, kv_here, 1)
    keys_rot = jnp.repeat(rotate(key_pick).astype(jnp.bfloat16), repeat_count, axis=1)
    values = jnp.repeat(value_pick, repeat_count, axis=1)
    scores = jnp.einsum(
        "qhd,khd->hqk", queries, keys_rot, preferred_element_type=jnp.float32
    ) * HD ** (-0.5)
    causal = jnp.arange(length)[:, None] >= jnp.arange(length)[None, :]
    scores = jnp.where(causal[None], scores, -jnp.inf)
    probabilities = jax.nn.softmax(scores, axis=-1).astype(jnp.bfloat16)
    context = jnp.einsum("hqk,khd->qhd", probabilities, values, preferred_element_type=jnp.float32)
    head_ids = first_head + jnp.arange(heads_here)
    context = jnp.where((head_ids < active)[None, :, None], context, 0.0).astype(jnp.bfloat16)
    return context.reshape(length, query_width)


def per_device(
    hidden_in,
    attn_gain,
    w_query,
    w_key,
    w_value,
    w_out,
    ffn_gain,
    w_gate,
    w_up,
    w_down,
    ffn_blocks,
    heads_on,
):
    section_count = lax.axis_size("section")
    section_index = lax.axis_index("section")
    model_count = lax.axis_size("mp")
    model_index = lax.axis_index("mp")
    micro_total = ffn_blocks.shape[0]
    per_section = hidden_in.shape[0]
    length = hidden_in.shape[2]
    model_width = hidden_in.shape[3]
    local_rows = length // model_count
    units_here = w_gate.shape[2]
    query_width = w_query.shape[2]
    key_width = w_key.shape[2]
    first_head = model_index * (query_width // HD)
    first_unit = model_index * units_here
    joined_qkv = [jnp.concatenate([w_query[0], w_key[0], w_value[0]], axis=1)]
    joined_pair = [jnp.concatenate([w_gate[0], w_up[0]], axis=1)]

    def gated(pre_act, block_count):
        gate_part = pre_act[:, :units_here]
        up_part = pre_act[:, units_here:]
        unit_ids = first_unit + jnp.arange(units_here)
        return jnp.where(
            (unit_ids < BLOCK * block_count)[None, :], jax.nn.silu(gate_part) * up_part, 0.0
        ).astype(jnp.bfloat16)

    def layer_rows(carried, layer_pos, active, block_count):
        residual = carried.astype(jnp.float32)
        normed = rms_scale(residual, attn_gain[layer_pos]).astype(jnp.bfloat16)
        projected = jnp.dot(
            collect(normed, "mp", 0), joined_qkv[layer_pos], preferred_element_type=jnp.float32
        )
        context = attend_local(projected, query_width, key_width, active, first_head)
        attended = residual + summed_on_arrival(
            jnp.dot(context, w_out[layer_pos], preferred_element_type=jnp.float32).astype(
                jnp.bfloat16
            ),
            "mp",
            0,
        )
        normed_ffn = rms_scale(attended, ffn_gain[layer_pos]).astype(jnp.bfloat16)
        hidden = gated(
            jnp.dot(
                collect(normed_ffn, "mp", 0),
                joined_pair[layer_pos],
                preferred_element_type=jnp.float32,
            ),
            block_count,
        )
        return (
            attended
            + summed_on_arrival(
                jnp.dot(hidden, w_down[layer_pos], preferred_element_type=jnp.float32).astype(
                    jnp.bfloat16
                ),
                "mp",
                0,
            )
        ).astype(jnp.bfloat16)

    def section_work(carried, moment, layer_fn):
        micro_index = jnp.clip(moment - section_index, 0, micro_total - 1)
        carried = layer_fn(carried, 0, heads_on[micro_index, 0], ffn_blocks[micro_index, 0])
        return carried

    def tick_step(moment, loop_carry):
        carried, slot_buffer = loop_carry
        cycle_index = moment // section_count
        incoming = lax.dynamic_index_in_dim(
            slot_buffer, jnp.minimum(cycle_index, per_section - 1), 0, keepdims=False
        )
        incoming = jnp.where(moment < micro_total, incoming, jnp.zeros_like(incoming))
        at_head = section_index == 0
        written = lax.dynamic_update_index_in_dim(
            slot_buffer, carried, jnp.maximum(cycle_index - 1, 0), 0
        )
        slot_buffer = jnp.where(at_head & (moment >= section_count), written, slot_buffer)
        carried = jnp.where(at_head, incoming, carried)
        carried = section_work(carried, moment, layer_rows)
        carried = passed_along(carried, "section", 1)
        slot_buffer = passed_along(slot_buffer, "section", -1)
        return (carried, slot_buffer)

    slot_start = hidden_in.reshape(per_section, length, model_width)
    slot_start = lax.dynamic_slice_in_dim(slot_start, model_index * local_rows, local_rows, 1)
    initial = jnp.zeros((local_rows, model_width), jnp.bfloat16)
    finished = lax.fori_loop(0, micro_total + section_count, tick_step, (initial, slot_start))
    result = finished[1]
    result = collect(result, "mp", 1)
    return result.reshape(hidden_in.shape)


def solution(mesh):
    return jax.shard_map(
        per_device,
        mesh=mesh,
        in_specs=(
            P(None, "section", None, None),
            P("section", None),
            P("section", None, "mp"),
            P("section", None, "mp"),
            P("section", None, "mp"),
            P("section", "mp", None),
            P("section", None),
            P("section", None, "mp"),
            P("section", None, "mp"),
            P("section", "mp", None),
            P(None, "section"),
            P(None, "section"),
        ),
        out_specs=P(None, "section", None, None),
        check_vma=False,
    )
```

profile of v0, /device:TPU:1, one launch (start us, length us, event | category | flops | bytes accessed | tf_op | source)
XLA Modules:
  0.0 910.3 jit_solution(10943014542577423044)
XLA Ops:
  15.2 877.5 %while.21 = (s32[]{:T(128)}, bf16[2,4096]{1,0:T(2,128)(2,1)S(1)}, bf16[1,2,4096]{2,1,0:T(2,128)(2,1)S(1)}, pred[]{:T(512)}, s32[]{:T(128)}, /*index=5*/s32[]{:T(...) while((s32[]{:T(128)}, bf16[2,4096]{1,0:T(2,128)(2,1)S(1)}, ...), condition=%wide.region_7.8_spmd, body=%wide.region_0.7_spmd.sunk | while | flops 977384448 | bytes 49139016 | solution.py:213
  27.5 10.3 %all-to-all-done = bf16[32,2,4096]{2,1,0:T(2,128)(2,1)S(1)} async-done(((bf16[32,2,4096]{2,1,0:T(2,128)(2,1)}), bf16[32,2,4096]{2,1,0:T(2,128)(2,1)S(1)}, u32[]{:S(2)}, u32[]{:S(2)}) %all-to-all-start) | async-done | bytes 524320 | tf_op jit(solution)/shard_map/while/body/eval_jaxpr/all_to_all | solution.py:36
  40.6 22.9 %all_gather.11 = bf16[1024,128]{1,0:T(8,128)(2,1)S(1)} all-gather(bf16[32,128]{1,0:T(8,128)(2,1)S(1)} %pad_maximum_fusion.4), channel_id=1, replica_groups=mesh['section'=4,'mp'=32] {'mp'}, dimensions={0}, use_global_device_ids=true | all-gather | bytes 270336 | tf_op jit(solution)/shard_map/while/body/eval_jaxpr/all_gather | solution.py:18
  71.9 11.6 %all-to-all-done.1 = bf16[32,2,4096]{2,1,0:T(2,128)(2,1)S(1)} async-done(((bf16[32,2,4096]{2,1,0:T(2,128)(2,1)}), bf16[32,2,4096]{2,1,0:T(2,128)(2,1)S(1)}, u32[]{:S(2)}, u32[]{:S(2)}) %all-to-all-start.1) | async-done | bytes 524320 | tf_op jit(solution)/shard_map/while/body/eval_jaxpr/all_to_all | solution.py:51
  136.6 10.3 %all-to-all-done = bf16[32,2,4096]{2,1,0:T(2,128)(2,1)S(1)} async-done(((bf16[32,2,4096]{2,1,0:T(2,128)(2,1)}), bf16[32,2,4096]{2,1,0:T(2,128)(2,1)S(1)}, u32[]{:S(2)}, u32[]{:S(2)}) %all-to-all-start) | async-done | bytes 524320 | tf_op jit(solution)/shard_map/while/body/eval_jaxpr/all_to_all | solution.py:36
  149.7 22.9 %all_gather.11 = bf16[1024,128]{1,0:T(8,128)(2,1)S(1)} all-gather(bf16[32,128]{1,0:T(8,128)(2,1)S(1)} %pad_maximum_fusion.4), channel_id=1, replica_groups=mesh['section'=4,'mp'=32] {'mp'}, dimensions={0}, use_global_device_ids=true | all-gather | bytes 270336 | tf_op jit(solution)/shard_map/while/body/eval_jaxpr/all_gather | solution.py:18
  181.0 11.6 %all-to-all-done.1 = bf16[32,2,4096]{2,1,0:T(2,128)(2,1)S(1)} async-done(((bf16[32,2,4096]{2,1,0:T(2,128)(2,1)}), bf16[32,2,4096]{2,1,0:T(2,128)(2,1)S(1)}, u32[]{:S(2)}, u32[]{:S(2)}) %all-to-all-start.1) | async-done | bytes 524320 | tf_op jit(solution)/shard_map/while/body/eval_jaxpr/all_to_all | solution.py:51
  245.7 10.3 %all-to-all-done = bf16[32,2,4096]{2,1,0:T(2,128)(2,1)S(1)} async-done(((bf16[32,2,4096]{2,1,0:T(2,128)(2,1)}), bf16[32,2,4096]{2,1,0:T(2,128)(2,1)S(1)}, u32[]{:S(2)}, u32[]{:S(2)}) %all-to-all-start) | async-done | bytes 524320 | tf_op jit(solution)/shard_map/while/body/eval_jaxpr/all_to_all | solution.py:36
  258.8 22.9 %all_gather.11 = bf16[1024,128]{1,0:T(8,128)(2,1)S(1)} all-gather(bf16[32,128]{1,0:T(8,128)(2,1)S(1)} %pad_maximum_fusion.4), channel_id=1, replica_groups=mesh['section'=4,'mp'=32] {'mp'}, dimensions={0}, use_global_device_ids=true | all-gather | bytes 270336 | tf_op jit(solution)/shard_map/while/body/eval_jaxpr/all_gather | solution.py:18
  290.1 11.6 %all-to-all-done.1 = bf16[32,2,4096]{2,1,0:T(2,128)(2,1)S(1)} async-done(((bf16[32,2,4096]{2,1,0:T(2,128)(2,1)}), bf16[32,2,4096]{2,1,0:T(2,128)(2,1)S(1)}, u32[]{:S(2)}, u32[]{:S(2)}) %all-to-all-start.1) | async-done | bytes 524320 | tf_op jit(solution)/shard_map/while/body/eval_jaxpr/all_to_all | solution.py:51
  331.8 11.1 %all-to-all-done.3 = bf16[32,2,4096]{2,1,0:T(2,128)(2,1)S(1)} async-done(((bf16[32,2,4096]{2,1,0:T(2,128)(2,1)}), bf16[32,2,4096]{2,1,0:T(2,128)(2,1)S(1)}, u32[]{:S(2)}, u32[]{:S(2)}) %all-to-all-start.3) | async-done | bytes 524320 | tf_op jit(solution)/shard_map/while/body/eval_jaxpr/all_to_all | solution.py:51
  354.8 10.3 %all-to-all-done = bf16[32,2,4096]{2,1,0:T(2,128)(2,1)S(1)} async-done(((bf16[32,2,4096]{2,1,0:T(2,128)(2,1)}), bf16[32,2,4096]{2,1,0:T(2,128)(2,1)S(1)}, u32[]{:S(2)}, u32[]{:S(2)}) %all-to-all-start) | async-done | bytes 524320 | tf_op jit(solution)/shard_map/while/body/eval_jaxpr/all_to_all | solution.py:36
  367.9 22.9 %all_gather.11 = bf16[1024,128]{1,0:T(8,128)(2,1)S(1)} all-gather(bf16[32,128]{1,0:T(8,128)(2,1)S(1)} %pad_maximum_fusion.4), channel_id=1, replica_groups=mesh['section'=4,'mp'=32] {'mp'}, dimensions={0}, use_global_device_ids=true | all-gather | bytes 270336 | tf_op jit(solution)/shard_map/while/body/eval_jaxpr/all_gather | solution.py:18
  399.2 11.6 %all-to-all-done.1 = bf16[32,2,4096]{2,1,0:T(2,128)(2,1)S(1)} async-done(((bf16[32,2,4096]{2,1,0:T(2,128)(2,1)}), bf16[32,2,4096]{2,1,0:T(2,128)(2,1)S(1)}, u32[]{:S(2)}, u32[]{:S(2)}) %all-to-all-start.1) | async-done | bytes 524320 | tf_op jit(solution)/shard_map/while/body/eval_jaxpr/all_to_all | solution.py:51
  440.6 11.4 %all-to-all-done.3 = bf16[32,2,4096]{2,1,0:T(2,128)(2,1)S(1)} async-done(((bf16[32,2,4096]{2,1,0:T(2,128)(2,1)}), bf16[32,2,4096]{2,1,0:T(2,128)(2,1)S(1)}, u32[]{:S(2)}, u32[]{:S(2)}) %all-to-all-start.3) | async-done | bytes 524320 | tf_op jit(solution)/shard_map/while/body/eval_jaxpr/all_to_all | solution.py:51
  463.9 10.3 %all-to-all-done = bf16[32,2,4096]{2,1,0:T(2,128)(2,1)S(1)} async-done(((bf16[32,2,4096]{2,1,0:T(2,128)(2,1)}), bf16[32,2,4096]{2,1,0:T(2,128)(2,1)S(1)}, u32[]{:S(2)}, u32[]{:S(2)}) %all-to-all-start) | async-done | bytes 524320 | tf_op jit(solution)/shard_map/while/body/eval_jaxpr/all_to_all | solution.py:36
  477.0 22.9 %all_gather.11 = bf16[1024,128]{1,0:T(8,128)(2,1)S(1)} all-gather(bf16[32,128]{1,0:T(8,128)(2,1)S(1)} %pad_maximum_fusion.4), channel_id=1, replica_groups=mesh['section'=4,'mp'=32] {'mp'}, dimensions={0}, use_global_device_ids=true | all-gather | bytes 270336 | tf_op jit(solution)/shard_map/while/body/eval_jaxpr/all_gather | solution.py:18
  508.3 11.6 %all-to-all-done.1 = bf16[32,2,4096]{2,1,0:T(2,128)(2,1)S(1)} async-done(((bf16[32,2,4096]{2,1,0:T(2,128)(2,1)}), bf16[32,2,4096]{2,1,0:T(2,128)(2,1)S(1)}, u32[]{:S(2)}, u32[]{:S(2)}) %all-to-all-start.1) | async-done | bytes 524320 | tf_op jit(solution)/shard_map/while/body/eval_jaxpr/all_to_all | solution.py:51
  549.7 11.4 %all-to-all-done.3 = bf16[32,2,4096]{2,1,0:T(2,128)(2,1)S(1)} async-done(((bf16[32,2,4096]{2,1,0:T(2,128)(2,1)}), bf16[32,2,4096]{2,1,0:T(2,128)(2,1)S(1)}, u32[]{:S(2)}, u32[]{:S(2)}) %all-to-all-start.3) | async-done | bytes 524320 | tf_op jit(solution)/shard_map/while/body/eval_jaxpr/all_to_all | solution.py:51
  573.0 10.3 %all-to-all-done = bf16[32,2,4096]{2,1,0:T(2,128)(2,1)S(1)} async-done(((bf16[32,2,4096]{2,1,0:T(2,128)(2,1)}), bf16[32,2,4096]{2,1,0:T(2,128)(2,1)S(1)}, u32[]{:S(2)}, u32[]{:S(2)}) %all-to-all-start) | async-done | bytes 524320 | tf_op jit(solution)/shard_map/while/body/eval_jaxpr/all_to_all | solution.py:36
  586.1 22.9 %all_gather.11 = bf16[1024,128]{1,0:T(8,128)(2,1)S(1)} all-gather(bf16[32,128]{1,0:T(8,128)(2,1)S(1)} %pad_maximum_fusion.4), channel_id=1, replica_groups=mesh['section'=4,'mp'=32] {'mp'}, dimensions={0}, use_global_device_ids=true | all-gather | bytes 270336 | tf_op jit(solution)/shard_map/while/body/eval_jaxpr/all_gather | solution.py:18
  617.4 11.6 %all-to-all-done.1 = bf16[32,2,4096]{2,1,0:T(2,128)(2,1)S(1)} async-done(((bf16[32,2,4096]{2,1,0:T(2,128)(2,1)}), bf16[32,2,4096]{2,1,0:T(2,128)(2,1)S(1)}, u32[]{:S(2)}, u32[]{:S(2)}) %all-to-all-start.1) | async-done | bytes 524320 | tf_op jit(solution)/shard_map/while/body/eval_jaxpr/all_to_all | solution.py:51
  658.8 11.4 %all-to-all-done.3 = bf16[32,2,4096]{2,1,0:T(2,128)(2,1)S(1)} async-done(((bf16[32,2,4096]{2,1,0:T(2,128)(2,1)}), bf16[32,2,4096]{2,1,0:T(2,128)(2,1)S(1)}, u32[]{:S(2)}, u32[]{:S(2)}) %all-to-all-start.3) | async-done | bytes 524320 | tf_op jit(solution)/shard_map/while/body/eval_jaxpr/all_to_all | solution.py:51
  682.1 10.3 %all-to-all-done = bf16[32,2,4096]{2,1,0:T(2,128)(2,1)S(1)} async-done(((bf16[32,2,4096]{2,1,0:T(2,128)(2,1)}), bf16[32,2,4096]{2,1,0:T(2,128)(2,1)S(1)}, u32[]{:S(2)}, u32[]{:S(2)}) %all-to-all-start) | async-done | bytes 524320 | tf_op jit(solution)/shard_map/while/body/eval_jaxpr/all_to_all | solution.py:36
  695.2 22.9 %all_gather.11 = bf16[1024,128]{1,0:T(8,128)(2,1)S(1)} all-gather(bf16[32,128]{1,0:T(8,128)(2,1)S(1)} %pad_maximum_fusion.4), channel_id=1, replica_groups=mesh['section'=4,'mp'=32] {'mp'}, dimensions={0}, use_global_device_ids=true | all-gather | bytes 270336 | tf_op jit(solution)/shard_map/while/body/eval_jaxpr/all_gather | solution.py:18
  726.5 11.6 %all-to-all-done.1 = bf16[32,2,4096]{2,1,0:T(2,128)(2,1)S(1)} async-done(((bf16[32,2,4096]{2,1,0:T(2,128)(2,1)}), bf16[32,2,4096]{2,1,0:T(2,128)(2,1)S(1)}, u32[]{:S(2)}, u32[]{:S(2)}) %all-to-all-start.1) | async-done | bytes 524320 | tf_op jit(solution)/shard_map/while/body/eval_jaxpr/all_to_all | solution.py:51
  767.9 11.4 %all-to-all-done.3 = bf16[32,2,4096]{2,1,0:T(2,128)(2,1)S(1)} async-done(((bf16[32,2,4096]{2,1,0:T(2,128)(2,1)}), bf16[32,2,4096]{2,1,0:T(2,128)(2,1)S(1)}, u32[]{:S(2)}, u32[]{:S(2)}) %all-to-all-start.3) | async-done | bytes 524320 | tf_op jit(solution)/shard_map/while/body/eval_jaxpr/all_to_all | solution.py:51
  791.2 10.3 %all-to-all-done = bf16[32,2,4096]{2,1,0:T(2,128)(2,1)S(1)} async-done(((bf16[32,2,4096]{2,1,0:T(2,128)(2,1)}), bf16[32,2,4096]{2,1,0:T(2,128)(2,1)S(1)}, u32[]{:S(2)}, u32[]{:S(2)}) %all-to-all-start) | async-done | bytes 524320 | tf_op jit(solution)/shard_map/while/body/eval_jaxpr/all_to_all | solution.py:36
  804.3 22.9 %all_gather.11 = bf16[1024,128]{1,0:T(8,128)(2,1)S(1)} all-gather(bf16[32,128]{1,0:T(8,128)(2,1)S(1)} %pad_maximum_fusion.4), channel_id=1, replica_groups=mesh['section'=4,'mp'=32] {'mp'}, dimensions={0}, use_global_device_ids=true | all-gather | bytes 270336 | tf_op jit(solution)/shard_map/while/body/eval_jaxpr/all_gather | solution.py:18
  835.6 11.6 %all-to-all-done.1 = bf16[32,2,4096]{2,1,0:T(2,128)(2,1)S(1)} async-done(((bf16[32,2,4096]{2,1,0:T(2,128)(2,1)}), bf16[32,2,4096]{2,1,0:T(2,128)(2,1)S(1)}, u32[]{:S(2)}, u32[]{:S(2)}) %all-to-all-start.1) | async-done | bytes 524320 | tf_op jit(solution)/shard_map/while/body/eval_jaxpr/all_to_all | solution.py:51
  877.0 11.4 %all-to-all-done.3 = bf16[32,2,4096]{2,1,0:T(2,128)(2,1)S(1)} async-done(((bf16[32,2,4096]{2,1,0:T(2,128)(2,1)}), bf16[32,2,4096]{2,1,0:T(2,128)(2,1)S(1)}, u32[]{:S(2)}, u32[]{:S(2)}) %all-to-all-start.3) | async-done | bytes 524320 | tf_op jit(solution)/shard_map/while/body/eval_jaxpr/all_to_all | solution.py:51
  893.2 16.2 %all_to_all.57 = bf16[32,1,2,4096]{3,2,1,0:T(2,128)(2,1)S(1)} all-to-all(bf16[32,1,2,4096]{3,2,1,0:T(2,128)(2,1)S(1)} %broadcast_in_dim.154), channel_id=1, replica_groups=mesh['section'=4,'mp'=32] {'mp'}, dimensions={0} | all-to-all | bytes 1048576 | tf_op jit(solution)/shard_map/all_to_all | solution.py:36
  (412 shorter events, 460.3 us)
Async XLA Ops:
  16.8 21.0 %all-to-all-start = ((bf16[32,2,4096]{2,1,0:T(2,128)(2,1)}), bf16[32,2,4096]{2,1,0:T(2,128)(2,1)S(1)}, u32[]{:S(2)}, u32[]{:S(2)}) async-start(bf16[32,2,4096]{2,1,0:T(2,128)(2,1)} %broadcast_in_dim.182), calls=%async_computation | async-start | bytes 1048576 | tf_op jit(solution)/shard_map/while/body/eval_jaxpr/all_to_all | solution.py:36
  67.4 16.1 %all-to-all-start.1 = ((bf16[32,2,4096]{2,1,0:T(2,128)(2,1)}), bf16[32,2,4096]{2,1,0:T(2,128)(2,1)S(1)}, u32[]{:S(2)}, u32[]{:S(2)}) async-start(bf16[32,2,4096]{2,1,0:T(2,128)(2,1)} %reshape.303), calls=%async_computation.1 | async-start | bytes 1048576 | tf_op jit(solution)/shard_map/while/body/eval_jaxpr/all_to_all | solution.py:51
  85.4 15.7 %all-to-all-start.2 = ((bf16[32,2,4096]{2,1,0:T(2,128)(2,1)}), bf16[32,2,4096]{2,1,0:T(2,128)(2,1)}, u32[]{:S(2)}, u32[]{:S(2)}) async-start(bf16[32,2,4096]{2,1,0:T(2,128)(2,1)} %broadcast_in_dim.183), calls=%async_computation.2 | async-start | bytes 1048576 | tf_op jit(solution)/shard_map/while/body/eval_jaxpr/all_to_all | solution.py:36
  109.4 15.2 %all-to-all-start.3 = ((bf16[32,2,4096]{2,1,0:T(2,128)(2,1)}), bf16[32,2,4096]{2,1,0:T(2,128)(2,1)S(1)}, u32[]{:S(2)}, u32[]{:S(2)}) async-start(bf16[32,2,4096]{2,1,0:T(2,128)(2,1)} %reshape.305), calls=%async_computation.3 | async-start | bytes 1048576 | tf_op jit(solution)/shard_map/while/body/eval_jaxpr/all_to_all | solution.py:51
  130.9 16.0 %all-to-all-start = ((bf16[32,2,4096]{2,1,0:T(2,128)(2,1)}), bf16[32,2,4096]{2,1,0:T(2,128)(2,1)S(1)}, u32[]{:S(2)}, u32[]{:S(2)}) async-start(bf16[32,2,4096]{2,1,0:T(2,128)(2,1)} %broadcast_in_dim.182), calls=%async_computation | async-start | bytes 1048576 | tf_op jit(solution)/shard_map/while/body/eval_jaxpr/all_to_all | solution.py:36
  176.5 16.1 %all-to-all-start.1 = ((bf16[32,2,4096]{2,1,0:T(2,128)(2,1)}), bf16[32,2,4096]{2,1,0:T(2,128)(2,1)S(1)}, u32[]{:S(2)}, u32[]{:S(2)}) async-start(bf16[32,2,4096]{2,1,0:T(2,128)(2,1)} %reshape.303), calls=%async_computation.1 | async-start | bytes 1048576 | tf_op jit(solution)/shard_map/while/body/eval_jaxpr/all_to_all | solution.py:51
  194.5 15.7 %all-to-all-start.2 = ((bf16[32,2,4096]{2,1,0:T(2,128)(2,1)}), bf16[32,2,4096]{2,1,0:T(2,128)(2,1)}, u32[]{:S(2)}, u32[]{:S(2)}) async-start(bf16[32,2,4096]{2,1,0:T(2,128)(2,1)} %broadcast_in_dim.183), calls=%async_computation.2 | async-start | bytes 1048576 | tf_op jit(solution)/shard_map/while/body/eval_jaxpr/all_to_all | solution.py:36
  218.6 15.2 %all-to-all-start.3 = ((bf16[32,2,4096]{2,1,0:T(2,128)(2,1)}), bf16[32,2,4096]{2,1,0:T(2,128)(2,1)S(1)}, u32[]{:S(2)}, u32[]{:S(2)}) async-start(bf16[32,2,4096]{2,1,0:T(2,128)(2,1)} %reshape.305), calls=%async_computation.3 | async-start | bytes 1048576 | tf_op jit(solution)/shard_map/while/body/eval_jaxpr/all_to_all | solution.py:51
  239.6 16.4 %all-to-all-start = ((bf16[32,2,4096]{2,1,0:T(2,128)(2,1)}), bf16[32,2,4096]{2,1,0:T(2,128)(2,1)S(1)}, u32[]{:S(2)}, u32[]{:S(2)}) async-start(bf16[32,2,4096]{2,1,0:T(2,128)(2,1)} %broadcast_in_dim.182), calls=%async_computation | async-start | bytes 1048576 | tf_op jit(solution)/shard_map/while/body/eval_jaxpr/all_to_all | solution.py:36
  285.6 16.1 %all-to-all-start.1 = ((bf16[32,2,4096]{2,1,0:T(2,128)(2,1)}), bf16[32,2,4096]{2,1,0:T(2,128)(2,1)S(1)}, u32[]{:S(2)}, u32[]{:S(2)}) async-start(bf16[32,2,4096]{2,1,0:T(2,128)(2,1)} %reshape.303), calls=%async_computation.1 | async-start | bytes 1048576 | tf_op jit(solution)/shard_map/while/body/eval_jaxpr/all_to_all | solution.py:51
  303.6 15.7 %all-to-all-start.2 = ((bf16[32,2,4096]{2,1,0:T(2,128)(2,1)}), bf16[32,2,4096]{2,1,0:T(2,128)(2,1)}, u32[]{:S(2)}, u32[]{:S(2)}) async-start(bf16[32,2,4096]{2,1,0:T(2,128)(2,1)} %broadcast_in_dim.183), calls=%async_computation.2 | async-start | bytes 1048576 | tf_op jit(solution)/shard_map/while/body/eval_jaxpr/all_to_all | solution.py:36
  327.7 15.2 %all-to-all-start.3 = ((bf16[32,2,4096]{2,1,0:T(2,128)(2,1)}), bf16[32,2,4096]{2,1,0:T(2,128)(2,1)S(1)}, u32[]{:S(2)}, u32[]{:S(2)}) async-start(bf16[32,2,4096]{2,1,0:T(2,128)(2,1)} %reshape.305), calls=%async_computation.3 | async-start | bytes 1048576 | tf_op jit(solution)/shard_map/while/body/eval_jaxpr/all_to_all | solution.py:51
  348.7 16.4 %all-to-all-start = ((bf16[32,2,4096]{2,1,0:T(2,128)(2,1)}), bf16[32,2,4096]{2,1,0:T(2,128)(2,1)S(1)}, u32[]{:S(2)}, u32[]{:S(2)}) async-start(bf16[32,2,4096]{2,1,0:T(2,128)(2,1)} %broadcast_in_dim.182), calls=%async_computation | async-start | bytes 1048576 | tf_op jit(solution)/shard_map/while/body/eval_jaxpr/all_to_all | solution.py:36
  394.7 16.1 %all-to-all-start.1 = ((bf16[32,2,4096]{2,1,0:T(2,128)(2,1)}), bf16[32,2,4096]{2,1,0:T(2,128)(2,1)S(1)}, u32[]{:S(2)}, u32[]{:S(2)}) async-start(bf16[32,2,4096]{2,1,0:T(2,128)(2,1)} %reshape.303), calls=%async_computation.1 | async-start | bytes 1048576 | tf_op jit(solution)/shard_map/while/body/eval_jaxpr/all_to_all | solution.py:51
  412.7 15.7 %all-to-all-start.2 = ((bf16[32,2,4096]{2,1,0:T(2,128)(2,1)}), bf16[32,2,4096]{2,1,0:T(2,128)(2,1)}, u32[]{:S(2)}, u32[]{:S(2)}) async-start(bf16[32,2,4096]{2,1,0:T(2,128)(2,1)} %broadcast_in_dim.183), calls=%async_computation.2 | async-start | bytes 1048576 | tf_op jit(solution)/shard_map/while/body/eval_jaxpr/all_to_all | solution.py:36
  436.8 15.2 %all-to-all-start.3 = ((bf16[32,2,4096]{2,1,0:T(2,128)(2,1)}), bf16[32,2,4096]{2,1,0:T(2,128)(2,1)S(1)}, u32[]{:S(2)}, u32[]{:S(2)}) async-start(bf16[32,2,4096]{2,1,0:T(2,128)(2,1)} %reshape.305), calls=%async_computation.3 | async-start | bytes 1048576 | tf_op jit(solution)/shard_map/while/body/eval_jaxpr/all_to_all | solution.py:51
  457.8 16.4 %all-to-all-start = ((bf16[32,2,4096]{2,1,0:T(2,128)(2,1)}), bf16[32,2,4096]{2,1,0:T(2,128)(2,1)S(1)}, u32[]{:S(2)}, u32[]{:S(2)}) async-start(bf16[32,2,4096]{2,1,0:T(2,128)(2,1)} %broadcast_in_dim.182), calls=%async_computation | async-start | bytes 1048576 | tf_op jit(solution)/shard_map/while/body/eval_jaxpr/all_to_all | solution.py:36
  503.8 16.1 %all-to-all-start.1 = ((bf16[32,2,4096]{2,1,0:T(2,128)(2,1)}), bf16[32,2,4096]{2,1,0:T(2,128)(2,1)S(1)}, u32[]{:S(2)}, u32[]{:S(2)}) async-start(bf16[32,2,4096]{2,1,0:T(2,128)(2,1)} %reshape.303), calls=%async_computation.1 | async-start | bytes 1048576 | tf_op jit(solution)/shard_map/while/body/eval_jaxpr/all_to_all | solution.py:51
  521.8 15.7 %all-to-all-start.2 = ((bf16[32,2,4096]{2,1,0:T(2,128)(2,1)}), bf16[32,2,4096]{2,1,0:T(2,128)(2,1)}, u32[]{:S(2)}, u32[]{:S(2)}) async-start(bf16[32,2,4096]{2,1,0:T(2,128)(2,1)} %broadcast_in_dim.183), calls=%async_computation.2 | async-start | bytes 1048576 | tf_op jit(solution)/shard_map/while/body/eval_jaxpr/all_to_all | solution.py:36
  545.9 15.2 %all-to-all-start.3 = ((bf16[32,2,4096]{2,1,0:T(2,128)(2,1)}), bf16[32,2,4096]{2,1,0:T(2,128)(2,1)S(1)}, u32[]{:S(2)}, u32[]{:S(2)}) async-start(bf16[32,2,4096]{2,1,0:T(2,128)(2,1)} %reshape.305), calls=%async_computation.3 | async-start | bytes 1048576 | tf_op jit(solution)/shard_map/while/body/eval_jaxpr/all_to_all | solution.py:51
  566.9 16.4 %all-to-all-start = ((bf16[32,2,4096]{2,1,0:T(2,128)(2,1)}), bf16[32,2,4096]{2,1,0:T(2,128)(2,1)S(1)}, u32[]{:S(2)}, u32[]{:S(2)}) async-start(bf16[32,2,4096]{2,1,0:T(2,128)(2,1)} %broadcast_in_dim.182), calls=%async_computation | async-start | bytes 1048576 | tf_op jit(solution)/shard_map/while/body/eval_jaxpr/all_to_all | solution.py:36
  612.9 16.1 %all-to-all-start.1 = ((bf16[32,2,4096]{2,1,0:T(2,128)(2,1)}), bf16[32,2,4096]{2,1,0:T(2,128)(2,1)S(1)}, u32[]{:S(2)}, u32[]{:S(2)}) async-start(bf16[32,2,4096]{2,1,0:T(2,128)(2,1)} %reshape.303), calls=%async_computation.1 | async-start | bytes 1048576 | tf_op jit(solution)/shard_map/while/body/eval_jaxpr/all_to_all | solution.py:51
  630.9 15.7 %all-to-all-start.2 = ((bf16[32,2,4096]{2,1,0:T(2,128)(2,1)}), bf16[32,2,4096]{2,1,0:T(2,128)(2,1)}, u32[]{:S(2)}, u32[]{:S(2)}) async-start(bf16[32,2,4096]{2,1,0:T(2,128)(2,1)} %broadcast_in_dim.183), calls=%async_computation.2 | async-start | bytes 1048576 | tf_op jit(solution)/shard_map/while/body/eval_jaxpr/all_to_all | solution.py:36
  655.0 15.2 %all-to-all-start.3 = ((bf16[32,2,4096]{2,1,0:T(2,128)(2,1)}), bf16[32,2,4096]{2,1,0:T(2,128)(2,1)S(1)}, u32[]{:S(2)}, u32[]{:S(2)}) async-start(bf16[32,2,4096]{2,1,0:T(2,128)(2,1)} %reshape.305), calls=%async_computation.3 | async-start | bytes 1048576 | tf_op jit(solution)/shard_map/while/body/eval_jaxpr/all_to_all | solution.py:51
  676.0 16.4 %all-to-all-start = ((bf16[32,2,4096]{2,1,0:T(2,128)(2,1)}), bf16[32,2,4096]{2,1,0:T(2,128)(2,1)S(1)}, u32[]{:S(2)}, u32[]{:S(2)}) async-start(bf16[32,2,4096]{2,1,0:T(2,128)(2,1)} %broadcast_in_dim.182), calls=%async_computation | async-start | bytes 1048576 | tf_op jit(solution)/shard_map/while/body/eval_jaxpr/all_to_all | solution.py:36
  722.0 16.1 %all-to-all-start.1 = ((bf16[32,2,4096]{2,1,0:T(2,128)(2,1)}), bf16[32,2,4096]{2,1,0:T(2,128)(2,1)S(1)}, u32[]{:S(2)}, u32[]{:S(2)}) async-start(bf16[32,2,4096]{2,1,0:T(2,128)(2,1)} %reshape.303), calls=%async_computation.1 | async-start | bytes 1048576 | tf_op jit(solution)/shard_map/while/body/eval_jaxpr/all_to_all | solution.py:51
  740.0 15.7 %all-to-all-start.2 = ((bf16[32,2,4096]{2,1,0:T(2,128)(2,1)}), bf16[32,2,4096]{2,1,0:T(2,128)(2,1)}, u32[]{:S(2)}, u32[]{:S(2)}) async-start(bf16[32,2,4096]{2,1,0:T(2,128)(2,1)} %broadcast_in_dim.183), calls=%async_computation.2 | async-start | bytes 1048576 | tf_op jit(solution)/shard_map/while/body/eval_jaxpr/all_to_all | solution.py:36
  764.1 15.2 %all-to-all-start.3 = ((bf16[32,2,4096]{2,1,0:T(2,128)(2,1)}), bf16[32,2,4096]{2,1,0:T(2,128)(2,1)S(1)}, u32[]{:S(2)}, u32[]{:S(2)}) async-start(bf16[32,2,4096]{2,1,0:T(2,128)(2,1)} %reshape.305), calls=%async_computation.3 | async-start | bytes 1048576 | tf_op jit(solution)/shard_map/while/body/eval_jaxpr/all_to_all | solution.py:51
  785.1 16.4 %all-to-all-start = ((bf16[32,2,4096]{2,1,0:T(2,128)(2,1)}), bf16[32,2,4096]{2,1,0:T(2,128)(2,1)S(1)}, u32[]{:S(2)}, u32[]{:S(2)}) async-start(bf16[32,2,4096]{2,1,0:T(2,128)(2,1)} %broadcast_in_dim.182), calls=%async_computation | async-start | bytes 1048576 | tf_op jit(solution)/shard_map/while/body/eval_jaxpr/all_to_all | solution.py:36
  831.1 16.1 %all-to-all-start.1 = ((bf16[32,2,4096]{2,1,0:T(2,128)(2,1)}), bf16[32,2,4096]{2,1,0:T(2,128)(2,1)S(1)}, u32[]{:S(2)}, u32[]{:S(2)}) async-start(bf16[32,2,4096]{2,1,0:T(2,128)(2,1)} %reshape.303), calls=%async_computation.1 | async-start | bytes 1048576 | tf_op jit(solution)/shard_map/while/body/eval_jaxpr/all_to_all | solution.py:51
  849.1 15.7 %all-to-all-start.2 = ((bf16[32,2,4096]{2,1,0:T(2,128)(2,1)}), bf16[32,2,4096]{2,1,0:T(2,128)(2,1)}, u32[]{:S(2)}, u32[]{:S(2)}) async-start(bf16[32,2,4096]{2,1,0:T(2,128)(2,1)} %broadcast_in_dim.183), calls=%async_computation.2 | async-start | bytes 1048576 | tf_op jit(solution)/shard_map/while/body/eval_jaxpr/all_to_all | solution.py:36
  873.2 15.2 %all-to-all-start.3 = ((bf16[32,2,4096]{2,1,0:T(2,128)(2,1)}), bf16[32,2,4096]{2,1,0:T(2,128)(2,1)S(1)}, u32[]{:S(2)}, u32[]{:S(2)}) async-start(bf16[32,2,4096]{2,1,0:T(2,128)(2,1)} %reshape.305), calls=%async_computation.3 | async-start | bytes 1048576 | tf_op jit(solution)/shard_map/while/body/eval_jaxpr/all_to_all | solution.py:51
  (29 other events, 184.8 us)
where the time goes:
time: 915 us; the launch traced here: 910 us
  waiting for transfers between devices  371 us (41%)
  blocking collectives  200 us (22%)
  starting transfers between devices  150 us (16%)
  matrix products  74.9 us (8%)
  local copies, waits for them, and re-layouts  73 us (8%)
  other arithmetic  34.3 us (4%)
    all_gather x8, blocking collectives, rows_first(): out = lax.all_gather(both, axis, axis=0, tiled=True)  184 us
    all_to_all x16, waiting for transfers between devices, summed_on_arrival(): lax.all_to_all(in_blocks(array, dim, peers), axis, 0, 0, tiled=True)  179 us
    all_to_all x16, waiting for transfers between devices, sent_to_all(): return lax.all_to_all(copies, axis, split_axis=0, concat_axis=0, tiled=True)  163 us
    all_to_all x16, starting transfers between devices, sent_to_all(): return lax.all_to_all(copies, axis, split_axis=0, concat_axis=0, tiled=True)  77.6 us
    all_to_all x16, starting transfers between devices, summed_on_arrival(): lax.all_to_all(in_blocks(array, dim, peers), axis, 0, 0, tiled=True)  65.5 us
    dot_general x8, matrix products, layer_rows(): jnp.dot(collect(normed_ffn, 'mp', 0), joined_pair[layer_pos], preferred_e...  40.8 us
    ppermute x16, waiting for transfers between devices, passed_along(): lax.ppermute(array, axis, [(i, (i + by) % peers) for i in range(peers)])  29.3 us
    broadcast_in_dim x17, local copies, waits for them, and re-layouts, sent_to_all(): copies = jnp.broadcast_to(array, (lax.axis_size(axis), *array.shape))  20.8 us
  transfers between devices with their start and end apart: 48, of which 40 were waited for; matrix products, arithmetic and copies ran while one was open for 2% of the time, Pallas kernels for 0%

commit v1 on v0

--- a/solution.py
+++ b/solution.py
@@ -15,7 +15,8 @@
     turned = [jnp.moveaxis(a, dim, 0) for a, dim in zip(arrays, dims)]
     widths = [t[0].size for t in turned]
     both = jnp.concatenate([t.reshape(-1, w) for t, w in zip(turned, widths)], axis=1)
-    out = lax.all_gather(both, axis, axis=0, tiled=True)
+    sent = jnp.stack([both] * lax.axis_size(axis))
+    out = jnp.concatenate(lax.all_to_all(sent, axis, 0, 0), axis=0)
     pieces = jnp.split(out, [sum(widths[:k]) for k in range(1, len(widths))], axis=1)
     return tuple(
         (

time: 915 us -> 825 us (0.902)
  blocking collectives: 200 us -> 150 us
  waiting for transfers between devices: 371 us -> 350 us
  starting transfers between devices: 150 us -> 131 us
    all_gather x8 -> x0, blocking collectives: 184 us -> none  [rows_first(): out = lax.all_gather(both, axis, axis=0, tiled=True)]
    all_to_all x1 -> x9, blocking collectives: 16.2 us -> 150 us  [sent_to_all(): return lax.all_to_all(copies, axis, split_axis=0, concat_axis=0, tiled=True)]
    all_to_all x16 -> x8, waiting for transfers between devices: 163 us -> 80 us  [sent_to_all(): return lax.all_to_all(copies, axis, split_axis=0, concat_axis=0, tiled=True)]
    all_to_all x0 -> x8, waiting for transfers between devices: none -> 61.2 us  [rows_first(): out = jnp.concatenate(lax.all_to_all(sent, axis, 0, 0), axis=0)]
    all_to_all x16 -> x8, starting transfers between devices: 77.6 us -> 35.2 us  [sent_to_all(): return lax.all_to_all(copies, axis, split_axis=0, concat_axis=0, tiled=True)]
    all_to_all x0 -> x8, starting transfers between devices: none -> 29.3 us  [rows_first(): out = jnp.concatenate(lax.all_to_all(sent, axis, 0, 0), axis=0)]
where the time goes in v1:
time: 825 us; the launch traced here: 820 us
  waiting for transfers between devices  350 us (42%)
  blocking collectives  150 us (18%)
  starting transfers between devices  131 us (16%)
  matrix products  74.9 us (9%)
  local copies, waits for them, and re-layouts  72.6 us (9%)
  other arithmetic  34.4 us (4%)
    all_to_all x16, waiting for transfers between devices, summed_on_arrival(): lax.all_to_all(in_blocks(array, dim, peers), axis, 0, 0, tiled=True)  180 us
    all_to_all x9, blocking collectives, sent_to_all(): return lax.all_to_all(copies, axis, split_axis=0, concat_axis=0, tiled=True)  150 us
    all_to_all x8, waiting for transfers between devices, sent_to_all(): return lax.all_to_all(copies, axis, split_axis=0, concat_axis=0, tiled=True)  80 us
    all_to_all x8, waiting for transfers between devices, rows_first(): out = jnp.concatenate(lax.all_to_all(sent, axis, 0, 0), axis=0)  61.2 us
    all_to_all x16, starting transfers between devices, summed_on_arrival(): lax.all_to_all(in_blocks(array, dim, peers), axis, 0, 0, tiled=True)  59.3 us
    dot_general x8, matrix products, layer_rows(): jnp.dot(collect(normed_ffn, 'mp', 0), joined_pair[layer_pos], preferred_e...  40.8 us
    all_to_all x8, starting transfers between devices, sent_to_all(): return lax.all_to_all(copies, axis, split_axis=0, concat_axis=0, tiled=True)  35.2 us
    ppermute x16, waiting for transfers between devices, passed_along(): lax.ppermute(array, axis, [(i, (i + by) % peers) for i in range(peers)])  29.3 us
  transfers between devices with their start and end apart: 48, of which 40 were waited for; matrix products, arithmetic and copies ran while one was open for 2% of the time, Pallas kernels for 0%

profile of v1, /device:TPU:1, one launch (start us, length us, event | category | flops | bytes accessed | tf_op | source)
XLA Modules:
  0.0 820.0 jit_solution(14281305434111085855)
XLA Ops:
  15.2 787.2 %while.21 = (s32[]{:T(128)}, bf16[2,4096]{1,0:T(2,128)(2,1)S(1)}, bf16[1,2,4096]{2,1,0:T(2,128)(2,1)S(1)}, pred[]{:T(512)}, s32[]{:T(128)}, /*index=5*/s32[]{:T(...) while((s32[]{:T(128)}, bf16[2,4096]{1,0:T(2,128)(2,1)S(1)}, ...), condition=%wide.region_7.8_spmd, body=%wide.region_0.7_spmd.sunk | while | flops 977384448 | bytes 49401160 | solution.py:214
  16.0 20.8 %all_to_all.71 = bf16[32,2,4096]{2,1,0:T(2,128)(2,1)S(1)} all-to-all(bf16[32,2,4096]{2,1,0:T(2,128)(2,1)S(1)} %broadcast_in_dim.182), channel_id=1, replica_groups=mesh['section'=4,'mp'=32] {'mp'}, dimensions={0} | all-to-all | bytes 1048576 | tf_op jit(solution)/shard_map/while/body/eval_jaxpr/all_to_all | solution.py:37
  60.5 11.7 %all-to-all-done.2 = bf16[32,2,4096]{2,1,0:T(2,128)(2,1)S(1)} async-done(((bf16[32,2,4096]{2,1,0:T(2,128)(2,1)}), bf16[32,2,4096]{2,1,0:T(2,128)(2,1)S(1)}, u32[]{:S(2)}, u32[]{:S(2)}) %all-to-all-start.2) | async-done | bytes 524320 | tf_op jit(solution)/shard_map/while/body/eval_jaxpr/all_to_all | solution.py:52
  79.8 10.0 %all-to-all-done.3 = bf16[32,2,4096]{2,1,0:T(2,128)(2,1)} async-done(((bf16[32,2,4096]{2,1,0:T(2,128)(2,1)}), bf16[32,2,4096]{2,1,0:T(2,128)(2,1)}, u32[]{:S(2)}, u32[]{:S(2)}) %all-to-all-start.3) | async-done | bytes 524320 | tf_op jit(solution)/shard_map/while/body/eval_jaxpr/all_to_all | solution.py:37
  118.8 15.7 %all_to_all.71 = bf16[32,2,4096]{2,1,0:T(2,128)(2,1)S(1)} all-to-all(bf16[32,2,4096]{2,1,0:T(2,128)(2,1)S(1)} %broadcast_in_dim.182), channel_id=1, replica_groups=mesh['section'=4,'mp'=32] {'mp'}, dimensions={0} | all-to-all | bytes 1048576 | tf_op jit(solution)/shard_map/while/body/eval_jaxpr/all_to_all | solution.py:37
  158.3 11.7 %all-to-all-done.2 = bf16[32,2,4096]{2,1,0:T(2,128)(2,1)S(1)} async-done(((bf16[32,2,4096]{2,1,0:T(2,128)(2,1)}), bf16[32,2,4096]{2,1,0:T(2,128)(2,1)S(1)}, u32[]{:S(2)}, u32[]{:S(2)}) %all-to-all-start.2) | async-done | bytes 524320 | tf_op jit(solution)/shard_map/while/body/eval_jaxpr/all_to_all | solution.py:52
  177.6 10.0 %all-to-all-done.3 = bf16[32,2,4096]{2,1,0:T(2,128)(2,1)} async-done(((bf16[32,2,4096]{2,1,0:T(2,128)(2,1)}), bf16[32,2,4096]{2,1,0:T(2,128)(2,1)}, u32[]{:S(2)}, u32[]{:S(2)}) %all-to-all-start.3) | async-done | bytes 524320 | tf_op jit(solution)/shard_map/while/body/eval_jaxpr/all_to_all | solution.py:37
  216.2 16.2 %all_to_all.71 = bf16[32,2,4096]{2,1,0:T(2,128)(2,1)S(1)} all-to-all(bf16[32,2,4096]{2,1,0:T(2,128)(2,1)S(1)} %broadcast_in_dim.182), channel_id=1, replica_groups=mesh['section'=4,'mp'=32] {'mp'}, dimensions={0} | all-to-all | bytes 1048576 | tf_op jit(solution)/shard_map/while/body/eval_jaxpr/all_to_all | solution.py:37
  256.1 11.7 %all-to-all-done.2 = bf16[32,2,4096]{2,1,0:T(2,128)(2,1)S(1)} async-done(((bf16[32,2,4096]{2,1,0:T(2,128)(2,1)}), bf16[32,2,4096]{2,1,0:T(2,128)(2,1)S(1)}, u32[]{:S(2)}, u32[]{:S(2)}) %all-to-all-start.2) | async-done | bytes 524320 | tf_op jit(solution)/shard_map/while/body/eval_jaxpr/all_to_all | solution.py:52
  275.4 10.0 %all-to-all-done.3 = bf16[32,2,4096]{2,1,0:T(2,128)(2,1)} async-done(((bf16[32,2,4096]{2,1,0:T(2,128)(2,1)}), bf16[32,2,4096]{2,1,0:T(2,128)(2,1)}, u32[]{:S(2)}, u32[]{:S(2)}) %all-to-all-start.3) | async-done | bytes 524320 | tf_op jit(solution)/shard_map/while/body/eval_jaxpr/all_to_all | solution.py:37
  297.9 11.1 %all-to-all-done.4 = bf16[32,2,4096]{2,1,0:T(2,128)(2,1)S(1)} async-done(((bf16[32,2,4096]{2,1,0:T(2,128)(2,1)}), bf16[32,2,4096]{2,1,0:T(2,128)(2,1)S(1)}, u32[]{:S(2)}, u32[]{:S(2)}) %all-to-all-start.4) | async-done | bytes 524320 | tf_op jit(solution)/shard_map/while/body/eval_jaxpr/all_to_all | solution.py:52
  314.1 16.2 %all_to_all.71 = bf16[32,2,4096]{2,1,0:T(2,128)(2,1)S(1)} all-to-all(bf16[32,2,4096]{2,1,0:T(2,128)(2,1)S(1)} %broadcast_in_dim.182), channel_id=1, replica_groups=mesh['section'=4,'mp'=32] {'mp'}, dimensions={0} | all-to-all | bytes 1048576 | tf_op jit(solution)/shard_map/while/body/eval_jaxpr/all_to_all | solution.py:37
  354.0 11.7 %all-to-all-done.2 = bf16[32,2,4096]{2,1,0:T(2,128)(2,1)S(1)} async-done(((bf16[32,2,4096]{2,1,0:T(2,128)(2,1)}), bf16[32,2,4096]{2,1,0:T(2,128)(2,1)S(1)}, u32[]{:S(2)}, u32[]{:S(2)}) %all-to-all-start.2) | async-done | bytes 524320 | tf_op jit(solution)/shard_map/while/body/eval_jaxpr/all_to_all | solution.py:52
  373.3 10.0 %all-to-all-done.3 = bf16[32,2,4096]{2,1,0:T(2,128)(2,1)} async-done(((bf16[32,2,4096]{2,1,0:T(2,128)(2,1)}), bf16[32,2,4096]{2,1,0:T(2,128)(2,1)}, u32[]{:S(2)}, u32[]{:S(2)}) %all-to-all-start.3) | async-done | bytes 524320 | tf_op jit(solution)/shard_map/while/body/eval_jaxpr/all_to_all | solution.py:37
  395.4 11.4 %all-to-all-done.4 = bf16[32,2,4096]{2,1,0:T(2,128)(2,1)S(1)} async-done(((bf16[32,2,4096]{2,1,0:T(2,128)(2,1)}), bf16[32,2,4096]{2,1,0:T(2,128)(2,1)S(1)}, u32[]{:S(2)}, u32[]{:S(2)}) %all-to-all-start.4) | async-done | bytes 524320 | tf_op jit(solution)/shard_map/while/body/eval_jaxpr/all_to_all | solution.py:52
  411.9 16.2 %all_to_all.71 = bf16[32,2,4096]{2,1,0:T(2,128)(2,1)S(1)} all-to-all(bf16[32,2,4096]{2,1,0:T(2,128)(2,1)S(1)} %broadcast_in_dim.182), channel_id=1, replica_groups=mesh['section'=4,'mp'=32] {'mp'}, dimensions={0} | all-to-all | bytes 1048576 | tf_op jit(solution)/shard_map/while/body/eval_jaxpr/all_to_all | solution.py:37
  451.8 11.7 %all-to-all-done.2 = bf16[32,2,4096]{2,1,0:T(2,128)(2,1)S(1)} async-done(((bf16[32,2,4096]{2,1,0:T(2,128)(2,1)}), bf16[32,2,4096]{2,1,0:T(2,128)(2,1)S(1)}, u32[]{:S(2)}, u32[]{:S(2)}) %all-to-all-start.2) | async-done | bytes 524320 | tf_op jit(solution)/shard_map/while/body/eval_jaxpr/all_to_all | solution.py:52
  471.1 10.0 %all-to-all-done.3 = bf16[32,2,4096]{2,1,0:T(2,128)(2,1)} async-done(((bf16[32,2,4096]{2,1,0:T(2,128)(2,1)}), bf16[32,2,4096]{2,1,0:T(2,128)(2,1)}, u32[]{:S(2)}, u32[]{:S(2)}) %all-to-all-start.3) | async-done | bytes 524320 | tf_op jit(solution)/shard_map/while/body/eval_jaxpr/all_to_all | solution.py:37
  493.2 11.4 %all-to-all-done.4 = bf16[32,2,4096]{2,1,0:T(2,128)(2,1)S(1)} async-done(((bf16[32,2,4096]{2,1,0:T(2,128)(2,1)}), bf16[32,2,4096]{2,1,0:T(2,128)(2,1)S(1)}, u32[]{:S(2)}, u32[]{:S(2)}) %all-to-all-start.4) | async-done | bytes 524320 | tf_op jit(solution)/shard_map/while/body/eval_jaxpr/all_to_all | solution.py:52
  509.7 16.2 %all_to_all.71 = bf16[32,2,4096]{2,1,0:T(2,128)(2,1)S(1)} all-to-all(bf16[32,2,4096]{2,1,0:T(2,128)(2,1)S(1)} %broadcast_in_dim.182), channel_id=1, replica_groups=mesh['section'=4,'mp'=32] {'mp'}, dimensions={0} | all-to-all | bytes 1048576 | tf_op jit(solution)/shard_map/while/body/eval_jaxpr/all_to_all | solution.py:37
  549.6 11.7 %all-to-all-done.2 = bf16[32,2,4096]{2,1,0:T(2,128)(2,1)S(1)} async-done(((bf16[32,2,4096]{2,1,0:T(2,128)(2,1)}), bf16[32,2,4096]{2,1,0:T(2,128)(2,1)S(1)}, u32[]{:S(2)}, u32[]{:S(2)}) %all-to-all-start.2) | async-done | bytes 524320 | tf_op jit(solution)/shard_map/while/body/eval_jaxpr/all_to_all | solution.py:52
  568.9 10.0 %all-to-all-done.3 = bf16[32,2,4096]{2,1,0:T(2,128)(2,1)} async-done(((bf16[32,2,4096]{2,1,0:T(2,128)(2,1)}), bf16[32,2,4096]{2,1,0:T(2,128)(2,1)}, u32[]{:S(2)}, u32[]{:S(2)}) %all-to-all-start.3) | async-done | bytes 524320 | tf_op jit(solution)/shard_map/while/body/eval_jaxpr/all_to_all | solution.py:37
  591.0 11.4 %all-to-all-done.4 = bf16[32,2,4096]{2,1,0:T(2,128)(2,1)S(1)} async-done(((bf16[32,2,4096]{2,1,0:T(2,128)(2,1)}), bf16[32,2,4096]{2,1,0:T(2,128)(2,1)S(1)}, u32[]{:S(2)}, u32[]{:S(2)}) %all-to-all-start.4) | async-done | bytes 524320 | tf_op jit(solution)/shard_map/while/body/eval_jaxpr/all_to_all | solution.py:52
  607.5 16.2 %all_to_all.71 = bf16[32,2,4096]{2,1,0:T(2,128)(2,1)S(1)} all-to-all(bf16[32,2,4096]{2,1,0:T(2,128)(2,1)S(1)} %broadcast_in_dim.182), channel_id=1, replica_groups=mesh['section'=4,'mp'=32] {'mp'}, dimensions={0} | all-to-all | bytes 1048576 | tf_op jit(solution)/shard_map/while/body/eval_jaxpr/all_to_all | solution.py:37
  647.4 11.7 %all-to-all-done.2 = bf16[32,2,4096]{2,1,0:T(2,128)(2,1)S(1)} async-done(((bf16[32,2,4096]{2,1,0:T(2,128)(2,1)}), bf16[32,2,4096]{2,1,0:T(2,128)(2,1)S(1)}, u32[]{:S(2)}, u32[]{:S(2)}) %all-to-all-start.2) | async-done | bytes 524320 | tf_op jit(solution)/shard_map/while/body/eval_jaxpr/all_to_all | solution.py:52
  666.7 10.0 %all-to-all-done.3 = bf16[32,2,4096]{2,1,0:T(2,128)(2,1)} async-done(((bf16[32,2,4096]{2,1,0:T(2,128)(2,1)}), bf16[32,2,4096]{2,1,0:T(2,128)(2,1)}, u32[]{:S(2)}, u32[]{:S(2)}) %all-to-all-start.3) | async-done | bytes 524320 | tf_op jit(solution)/shard_map/while/body/eval_jaxpr/all_to_all | solution.py:37
  688.9 11.4 %all-to-all-done.4 = bf16[32,2,4096]{2,1,0:T(2,128)(2,1)S(1)} async-done(((bf16[32,2,4096]{2,1,0:T(2,128)(2,1)}), bf16[32,2,4096]{2,1,0:T(2,128)(2,1)S(1)}, u32[]{:S(2)}, u32[]{:S(2)}) %all-to-all-start.4) | async-done | bytes 524320 | tf_op jit(solution)/shard_map/while/body/eval_jaxpr/all_to_all | solution.py:52
  705.3 16.2 %all_to_all.71 = bf16[32,2,4096]{2,1,0:T(2,128)(2,1)S(1)} all-to-all(bf16[32,2,4096]{2,1,0:T(2,128)(2,1)S(1)} %broadcast_in_dim.182), channel_id=1, replica_groups=mesh['section'=4,'mp'=32] {'mp'}, dimensions={0} | all-to-all | bytes 1048576 | tf_op jit(solution)/shard_map/while/body/eval_jaxpr/all_to_all | solution.py:37
  745.2 11.7 %all-to-all-done.2 = bf16[32,2,4096]{2,1,0:T(2,128)(2,1)S(1)} async-done(((bf16[32,2,4096]{2,1,0:T(2,128)(2,1)}), bf16[32,2,4096]{2,1,0:T(2,128)(2,1)S(1)}, u32[]{:S(2)}, u32[]{:S(2)}) %all-to-all-start.2) | async-done | bytes 524320 | tf_op jit(solution)/shard_map/while/body/eval_jaxpr/all_to_all | solution.py:52
  764.5 10.0 %all-to-all-done.3 = bf16[32,2,4096]{2,1,0:T(2,128)(2,1)} async-done(((bf16[32,2,4096]{2,1,0:T(2,128)(2,1)}), bf16[32,2,4096]{2,1,0:T(2,128)(2,1)}, u32[]{:S(2)}, u32[]{:S(2)}) %all-to-all-start.3) | async-done | bytes 524320 | tf_op jit(solution)/shard_map/while/body/eval_jaxpr/all_to_all | solution.py:37
  786.7 11.4 %all-to-all-done.4 = bf16[32,2,4096]{2,1,0:T(2,128)(2,1)S(1)} async-done(((bf16[32,2,4096]{2,1,0:T(2,128)(2,1)}), bf16[32,2,4096]{2,1,0:T(2,128)(2,1)S(1)}, u32[]{:S(2)}, u32[]{:S(2)}) %all-to-all-start.4) | async-done | bytes 524320 | tf_op jit(solution)/shard_map/while/body/eval_jaxpr/all_to_all | solution.py:52
  802.9 16.2 %all_to_all.70 = bf16[32,1,2,4096]{3,2,1,0:T(2,128)(2,1)S(1)} all-to-all(bf16[32,1,2,4096]{3,2,1,0:T(2,128)(2,1)S(1)} %broadcast_in_dim.154), channel_id=1, replica_groups=mesh['section'=4,'mp'=32] {'mp'}, dimensions={0} | all-to-all | bytes 1048576 | tf_op jit(solution)/shard_map/all_to_all | solution.py:37
  (420 shorter events, 421.8 us)
Async XLA Ops:
  56.7 15.4 %all-to-all-start.2 = ((bf16[32,2,4096]{2,1,0:T(2,128)(2,1)}), bf16[32,2,4096]{2,1,0:T(2,128)(2,1)S(1)}, u32[]{:S(2)}, u32[]{:S(2)}) async-start(bf16[32,2,4096]{2,1,0:T(2,128)(2,1)} %reshape.315), calls=%async_computation.2 | async-start | bytes 1048576 | tf_op jit(solution)/shard_map/while/body/eval_jaxpr/all_to_all | solution.py:52
  74.1 15.7 %all-to-all-start.3 = ((bf16[32,2,4096]{2,1,0:T(2,128)(2,1)}), bf16[32,2,4096]{2,1,0:T(2,128)(2,1)}, u32[]{:S(2)}, u32[]{:S(2)}) async-start(bf16[32,2,4096]{2,1,0:T(2,128)(2,1)} %broadcast_in_dim.183), calls=%async_computation.3 | async-start | bytes 1048576 | tf_op jit(solution)/shard_map/while/body/eval_jaxpr/all_to_all | solution.py:37
  98.2 15.2 %all-to-all-start.4 = ((bf16[32,2,4096]{2,1,0:T(2,128)(2,1)}), bf16[32,2,4096]{2,1,0:T(2,128)(2,1)S(1)}, u32[]{:S(2)}, u32[]{:S(2)}) async-start(bf16[32,2,4096]{2,1,0:T(2,128)(2,1)} %reshape.317), calls=%async_computation.4 | async-start | bytes 1048576 | tf_op jit(solution)/shard_map/while/body/eval_jaxpr/all_to_all | solution.py:52
  101.9 13.3 %collective-permute-start.1 = (bf16[1,2,4096]{2,1,0:T(2,128)(2,1)S(1)}, bf16[1,2,4096]{2,1,0:T(2,128)(2,1)S(1)}, u32[]{:S(2)}, u32[]{:S(2)}) collective-permute-start(bf16[1,2,4096]{2,1,0:T(2,128)(2,1)S(1)} %broadcast_select_fusion.5), channel_id=1, source_target_pairs={{0,96},{32,0},{64,32},{96,64},{1,97},{33,1},{65,33},{97,65},{2,98}... | collective-permute-start | bytes 49160 | tf_op jit(solution)/shard_map/while/body/eval_jaxpr/ppermute | solution.py:58
  138.2 12.6 %all-to-all-start.1 = ((bf16[32,32,128]{2,1,0:T(8,128)(2,1)}), bf16[32,32,128]{2,1,0:T(8,128)(2,1)S(1)}, u32[]{:S(2)}, u32[]{:S(2)}) async-start(bf16[32,32,128]{2,1,0:T(8,128)(2,1)} %stack.7), calls=%async_computation.1 | async-start | bytes 524288 | tf_op jit(solution)/shard_map/while/body/eval_jaxpr/all_to_all | solution.py:19
  154.5 15.4 %all-to-all-start.2 = ((bf16[32,2,4096]{2,1,0:T(2,128)(2,1)}), bf16[32,2,4096]{2,1,0:T(2,128)(2,1)S(1)}, u32[]{:S(2)}, u32[]{:S(2)}) async-start(bf16[32,2,4096]{2,1,0:T(2,128)(2,1)} %reshape.315), calls=%async_computation.2 | async-start | bytes 1048576 | tf_op jit(solution)/shard_map/while/body/eval_jaxpr/all_to_all | solution.py:52
  171.9 15.7 %all-to-all-start.3 = ((bf16[32,2,4096]{2,1,0:T(2,128)(2,1)}), bf16[32,2,4096]{2,1,0:T(2,128)(2,1)}, u32[]{:S(2)}, u32[]{:S(2)}) async-start(bf16[32,2,4096]{2,1,0:T(2,128)(2,1)} %broadcast_in_dim.183), calls=%async_computation.3 | async-start | bytes 1048576 | tf_op jit(solution)/shard_map/while/body/eval_jaxpr/all_to_all | solution.py:37
  196.0 15.2 %all-to-all-start.4 = ((bf16[32,2,4096]{2,1,0:T(2,128)(2,1)}), bf16[32,2,4096]{2,1,0:T(2,128)(2,1)S(1)}, u32[]{:S(2)}, u32[]{:S(2)}) async-start(bf16[32,2,4096]{2,1,0:T(2,128)(2,1)} %reshape.317), calls=%async_computation.4 | async-start | bytes 1048576 | tf_op jit(solution)/shard_map/while/body/eval_jaxpr/all_to_all | solution.py:52
  236.0 12.6 %all-to-all-start.1 = ((bf16[32,32,128]{2,1,0:T(8,128)(2,1)}), bf16[32,32,128]{2,1,0:T(8,128)(2,1)S(1)}, u32[]{:S(2)}, u32[]{:S(2)}) async-start(bf16[32,32,128]{2,1,0:T(8,128)(2,1)} %stack.7), calls=%async_computation.1 | async-start | bytes 524288 | tf_op jit(solution)/shard_map/while/body/eval_jaxpr/all_to_all | solution.py:19
  252.4 15.4 %all-to-all-start.2 = ((bf16[32,2,4096]{2,1,0:T(2,128)(2,1)}), bf16[32,2,4096]{2,1,0:T(2,128)(2,1)S(1)}, u32[]{:S(2)}, u32[]{:S(2)}) async-start(bf16[32,2,4096]{2,1,0:T(2,128)(2,1)} %reshape.315), calls=%async_computation.2 | async-start | bytes 1048576 | tf_op jit(solution)/shard_map/while/body/eval_jaxpr/all_to_all | solution.py:52
  269.8 15.7 %all-to-all-start.3 = ((bf16[32,2,4096]{2,1,0:T(2,128)(2,1)}), bf16[32,2,4096]{2,1,0:T(2,128)(2,1)}, u32[]{:S(2)}, u32[]{:S(2)}) async-start(bf16[32,2,4096]{2,1,0:T(2,128)(2,1)} %broadcast_in_dim.183), calls=%async_computation.3 | async-start | bytes 1048576 | tf_op jit(solution)/shard_map/while/body/eval_jaxpr/all_to_all | solution.py:37
  293.8 15.2 %all-to-all-start.4 = ((bf16[32,2,4096]{2,1,0:T(2,128)(2,1)}), bf16[32,2,4096]{2,1,0:T(2,128)(2,1)S(1)}, u32[]{:S(2)}, u32[]{:S(2)}) async-start(bf16[32,2,4096]{2,1,0:T(2,128)(2,1)} %reshape.317), calls=%async_computation.4 | async-start | bytes 1048576 | tf_op jit(solution)/shard_map/while/body/eval_jaxpr/all_to_all | solution.py:52
  333.8 12.6 %all-to-all-start.1 = ((bf16[32,32,128]{2,1,0:T(8,128)(2,1)}), bf16[32,32,128]{2,1,0:T(8,128)(2,1)S(1)}, u32[]{:S(2)}, u32[]{:S(2)}) async-start(bf16[32,32,128]{2,1,0:T(8,128)(2,1)} %stack.7), calls=%async_computation.1 | async-start | bytes 524288 | tf_op jit(solution)/shard_map/while/body/eval_jaxpr/all_to_all | solution.py:19
  350.2 15.4 %all-to-all-start.2 = ((bf16[32,2,4096]{2,1,0:T(2,128)(2,1)}), bf16[32,2,4096]{2,1,0:T(2,128)(2,1)S(1)}, u32[]{:S(2)}, u32[]{:S(2)}) async-start(bf16[32,2,4096]{2,1,0:T(2,128)(2,1)} %reshape.315), calls=%async_computation.2 | async-start | bytes 1048576 | tf_op jit(solution)/shard_map/while/body/eval_jaxpr/all_to_all | solution.py:52
  367.6 15.7 %all-to-all-start.3 = ((bf16[32,2,4096]{2,1,0:T(2,128)(2,1)}), bf16[32,2,4096]{2,1,0:T(2,128)(2,1)}, u32[]{:S(2)}, u32[]{:S(2)}) async-start(bf16[32,2,4096]{2,1,0:T(2,128)(2,1)} %broadcast_in_dim.183), calls=%async_computation.3 | async-start | bytes 1048576 | tf_op jit(solution)/shard_map/while/body/eval_jaxpr/all_to_all | solution.py:37
  391.6 15.2 %all-to-all-start.4 = ((bf16[32,2,4096]{2,1,0:T(2,128)(2,1)}), bf16[32,2,4096]{2,1,0:T(2,128)(2,1)S(1)}, u32[]{:S(2)}, u32[]{:S(2)}) async-start(bf16[32,2,4096]{2,1,0:T(2,128)(2,1)} %reshape.317), calls=%async_computation.4 | async-start | bytes 1048576 | tf_op jit(solution)/shard_map/while/body/eval_jaxpr/all_to_all | solution.py:52
  431.6 12.6 %all-to-all-start.1 = ((bf16[32,32,128]{2,1,0:T(8,128)(2,1)}), bf16[32,32,128]{2,1,0:T(8,128)(2,1)S(1)}, u32[]{:S(2)}, u32[]{:S(2)}) async-start(bf16[32,32,128]{2,1,0:T(8,128)(2,1)} %stack.7), calls=%async_computation.1 | async-start | bytes 524288 | tf_op jit(solution)/shard_map/while/body/eval_jaxpr/all_to_all | solution.py:19
  448.0 15.4 %all-to-all-start.2 = ((bf16[32,2,4096]{2,1,0:T(2,128)(2,1)}), bf16[32,2,4096]{2,1,0:T(2,128)(2,1)S(1)}, u32[]{:S(2)}, u32[]{:S(2)}) async-start(bf16[32,2,4096]{2,1,0:T(2,128)(2,1)} %reshape.315), calls=%async_computation.2 | async-start | bytes 1048576 | tf_op jit(solution)/shard_map/while/body/eval_jaxpr/all_to_all | solution.py:52
  465.4 15.7 %all-to-all-start.3 = ((bf16[32,2,4096]{2,1,0:T(2,128)(2,1)}), bf16[32,2,4096]{2,1,0:T(2,128)(2,1)}, u32[]{:S(2)}, u32[]{:S(2)}) async-start(bf16[32,2,4096]{2,1,0:T(2,128)(2,1)} %broadcast_in_dim.183), calls=%async_computation.3 | async-start | bytes 1048576 | tf_op jit(solution)/shard_map/while/body/eval_jaxpr/all_to_all | solution.py:37
  489.4 15.2 %all-to-all-start.4 = ((bf16[32,2,4096]{2,1,0:T(2,128)(2,1)}), bf16[32,2,4096]{2,1,0:T(2,128)(2,1)S(1)}, u32[]{:S(2)}, u32[]{:S(2)}) async-start(bf16[32,2,4096]{2,1,0:T(2,128)(2,1)} %reshape.317), calls=%async_computation.4 | async-start | bytes 1048576 | tf_op jit(solution)/shard_map/while/body/eval_jaxpr/all_to_all | solution.py:52
  529.5 12.6 %all-to-all-start.1 = ((bf16[32,32,128]{2,1,0:T(8,128)(2,1)}), bf16[32,32,128]{2,1,0:T(8,128)(2,1)S(1)}, u32[]{:S(2)}, u32[]{:S(2)}) async-start(bf16[32,32,128]{2,1,0:T(8,128)(2,1)} %stack.7), calls=%async_computation.1 | async-start | bytes 524288 | tf_op jit(solution)/shard_map/while/body/eval_jaxpr/all_to_all | solution.py:19
  545.8 15.4 %all-to-all-start.2 = ((bf16[32,2,4096]{2,1,0:T(2,128)(2,1)}), bf16[32,2,4096]{2,1,0:T(2,128)(2,1)S(1)}, u32[]{:S(2)}, u32[]{:S(2)}) async-start(bf16[32,2,4096]{2,1,0:T(2,128)(2,1)} %reshape.315), calls=%async_computation.2 | async-start | bytes 1048576 | tf_op jit(solution)/shard_map/while/body/eval_jaxpr/all_to_all | solution.py:52
  563.2 15.7 %all-to-all-start.3 = ((bf16[32,2,4096]{2,1,0:T(2,128)(2,1)}), bf16[32,2,4096]{2,1,0:T(2,128)(2,1)}, u32[]{:S(2)}, u32[]{:S(2)}) async-start(bf16[32,2,4096]{2,1,0:T(2,128)(2,1)} %broadcast_in_dim.183), calls=%async_computation.3 | async-start | bytes 1048576 | tf_op jit(solution)/shard_map/while/body/eval_jaxpr/all_to_all | solution.py:37
  587.2 15.2 %all-to-all-start.4 = ((bf16[32,2,4096]{2,1,0:T(2,128)(2,1)}), bf16[32,2,4096]{2,1,0:T(2,128)(2,1)S(1)}, u32[]{:S(2)}, u32[]{:S(2)}) async-start(bf16[32,2,4096]{2,1,0:T(2,128)(2,1)} %reshape.317), calls=%async_computation.4 | async-start | bytes 1048576 | tf_op jit(solution)/shard_map/while/body/eval_jaxpr/all_to_all | solution.py:52
  627.3 12.6 %all-to-all-start.1 = ((bf16[32,32,128]{2,1,0:T(8,128)(2,1)}), bf16[32,32,128]{2,1,0:T(8,128)(2,1)S(1)}, u32[]{:S(2)}, u32[]{:S(2)}) async-start(bf16[32,32,128]{2,1,0:T(8,128)(2,1)} %stack.7), calls=%async_computation.1 | async-start | bytes 524288 | tf_op jit(solution)/shard_map/while/body/eval_jaxpr/all_to_all | solution.py:19
  643.6 15.4 %all-to-all-start.2 = ((bf16[32,2,4096]{2,1,0:T(2,128)(2,1)}), bf16[32,2,4096]{2,1,0:T(2,128)(2,1)S(1)}, u32[]{:S(2)}, u32[]{:S(2)}) async-start(bf16[32,2,4096]{2,1,0:T(2,128)(2,1)} %reshape.315), calls=%async_computation.2 | async-start | bytes 1048576 | tf_op jit(solution)/shard_map/while/body/eval_jaxpr/all_to_all | solution.py:52
  661.0 15.7 %all-to-all-start.3 = ((bf16[32,2,4096]{2,1,0:T(2,128)(2,1)}), bf16[32,2,4096]{2,1,0:T(2,128)(2,1)}, u32[]{:S(2)}, u32[]{:S(2)}) async-start(bf16[32,2,4096]{2,1,0:T(2,128)(2,1)} %broadcast_in_dim.183), calls=%async_computation.3 | async-start | bytes 1048576 | tf_op jit(solution)/shard_map/while/body/eval_jaxpr/all_to_all | solution.py:37
  685.1 15.2 %all-to-all-start.4 = ((bf16[32,2,4096]{2,1,0:T(2,128)(2,1)}), bf16[32,2,4096]{2,1,0:T(2,128)(2,1)S(1)}, u32[]{:S(2)}, u32[]{:S(2)}) async-start(bf16[32,2,4096]{2,1,0:T(2,128)(2,1)} %reshape.317), calls=%async_computation.4 | async-start | bytes 1048576 | tf_op jit(solution)/shard_map/while/body/eval_jaxpr/all_to_all | solution.py:52
  725.1 12.6 %all-to-all-start.1 = ((bf16[32,32,128]{2,1,0:T(8,128)(2,1)}), bf16[32,32,128]{2,1,0:T(8,128)(2,1)S(1)}, u32[]{:S(2)}, u32[]{:S(2)}) async-start(bf16[32,32,128]{2,1,0:T(8,128)(2,1)} %stack.7), calls=%async_computation.1 | async-start | bytes 524288 | tf_op jit(solution)/shard_map/while/body/eval_jaxpr/all_to_all | solution.py:19
  741.5 15.4 %all-to-all-start.2 = ((bf16[32,2,4096]{2,1,0:T(2,128)(2,1)}), bf16[32,2,4096]{2,1,0:T(2,128)(2,1)S(1)}, u32[]{:S(2)}, u32[]{:S(2)}) async-start(bf16[32,2,4096]{2,1,0:T(2,128)(2,1)} %reshape.315), calls=%async_computation.2 | async-start | bytes 1048576 | tf_op jit(solution)/shard_map/while/body/eval_jaxpr/all_to_all | solution.py:52
  758.9 15.7 %all-to-all-start.3 = ((bf16[32,2,4096]{2,1,0:T(2,128)(2,1)}), bf16[32,2,4096]{2,1,0:T(2,128)(2,1)}, u32[]{:S(2)}, u32[]{:S(2)}) async-start(bf16[32,2,4096]{2,1,0:T(2,128)(2,1)} %broadcast_in_dim.183), calls=%async_computation.3 | async-start | bytes 1048576 | tf_op jit(solution)/shard_map/while/body/eval_jaxpr/all_to_all | solution.py:37
  782.9 15.2 %all-to-all-start.4 = ((bf16[32,2,4096]{2,1,0:T(2,128)(2,1)}), bf16[32,2,4096]{2,1,0:T(2,128)(2,1)S(1)}, u32[]{:S(2)}, u32[]{:S(2)}) async-start(bf16[32,2,4096]{2,1,0:T(2,128)(2,1)} %reshape.317), calls=%async_computation.4 | async-start | bytes 1048576 | tf_op jit(solution)/shard_map/while/body/eval_jaxpr/all_to_all | solution.py:52
  (29 other events, 184.1 us)
